TPU v7x, 16 devices: a 4x2x1 block of a 4x4x8 slice. The times are simulated.
16 devices in a mesh: dp: 2 (over y, z), vp: 8 (over x, core).
Axes of the slice: x: 4, y: 2, z: 1, core: 2. Of those that a mesh axis runs over, the one named last changes fastest.
The devices are a block of a 4x4x8 slice.
Arguments:
- hidden: bfloat16 [1024, 6144], P('dp'), parts along dimension 0
- w_head: bfloat16 [6144, 32768], P(None, 'vp')
- inv_temp: float32 [1024], P('dp'), parts along dimension 0
- target_ids: int32 [1024], P('dp'), parts along dimension 0
Outputs:
- output 1: float32 [1024, 32768], P(('dp', 'vp')), parts along dimension 0
- output 2: float32 [1024], P('dp'), parts along dimension 0
There are 2 independent parts. A program takes and returns all parts, laid end to end along the dimension named above; an argument that names none is the same for every part.
All inputs are finite; a program needn't handle non-finite values.
Results may differ from a plain program's by a relative error of at most 0.001.
Values are sent between devices in bfloat16 or wider.
A program may use at most 768 MiB of HBM per device.

v0:
```python
import jax
import jax.numpy as jnp
from jax import lax
from jax.sharding import PartitionSpec as P, NamedSharding


def solution(mesh):
    group_size = mesh.shape["vp"]

    def local_step(hidden, w_local, inv_temp, target_ids):
        group_index = lax.axis_index("vp")
        local_vocab = w_local.shape[1]
        logits = jnp.dot(hidden, w_local, preferred_element_type=jnp.float32)
        scaled = logits * inv_temp[:, None]
        local_max = jnp.max(scaled, axis=1)
        exp_vals = jnp.exp(scaled - local_max[:, None])
        local_sum = jnp.sum(exp_vals, axis=1)
        shard_stats = lax.all_gather(jnp.stack([local_max, local_sum]), "vp")
        global_max = jnp.max(shard_stats[:, 0], axis=0)
        global_sum = jnp.sum(shard_stats[:, 1] * jnp.exp(shard_stats[:, 0] - global_max[None, :]), axis=0)
        row_scale = jnp.exp(local_max - global_max) / global_sum
        local_cdf = jnp.cumsum(exp_vals * row_scale[:, None], axis=1)
        totals = lax.all_gather(local_cdf[:, -1], "vp")
        earlier = (jnp.arange(group_size) < group_index)[:, None]
        offset = jnp.sum(jnp.where(earlier, totals, 0.0), axis=0)
        cdf_cols = local_cdf + offset[:, None]
        local_ids = target_ids - group_index * local_vocab
        in_shard = (local_ids >= 0) & (local_ids < local_vocab)
        picked = jnp.take_along_axis(cdf_cols, jnp.clip(local_ids, 0, local_vocab - 1)[:, None], axis=1)[:, 0]
        cdf_at_target = lax.psum(jnp.where(in_shard, picked, 0.0), "vp")
        cdf_rows = lax.all_to_all(cdf_cols, "vp", 0, 1, tiled=True)
        return cdf_rows, cdf_at_target

    return jax.shard_map(
        local_step,
        mesh=mesh,
        in_specs=(P("dp", None), P(None, "vp"), P("dp"), P("dp")),
        out_specs=(P(("dp", "vp"), None), P("dp")),
        check_vma=False,
    )
```

profile of v0, /device:TPU:113, one launch (start us, length us, event | category | flops | bytes accessed | tf_op | source)
XLA Modules:
  0.0 275.2 jit_solution(832716213456017087)
XLA Ops:
  0.6 0.0 copy-start.1
  0.6 36.6 %multiply_reduce_fusion = (f32[512]{0:T(512)S(1)}, f32[512,4096]{1,0:T(8,128)S(1)}) fusion(f32[512]{0:T(512)} %param.6, bf16[512,6144]{1,0:T(8,128)(2,1)} %param.4, bf16[6144,4096]{1,0:T(8,128)(2,1)} %param.5), kind=kOutput, calls=%fused_computation.3 | convolution fusion | flops 25773998080 | bytes 65015808 | tf_op jit(solution)/shard_map/dot_general | solution.py:13
  37.2 0.0 copy-done.1
  37.2 1.8 fusion
  39.0 19.0 %all-gather.2 = f32[8,2,512]{2,1,0:T(2,128)S(1)} all-gather(f32[1,2,512]{2,1,0:T(2,128)S(1)} %maximum_bitcast_fusion), channel_id=2, replica_groups=mesh['dp'=2,'vp'=8] {'vp'}, dimensions={0}, use_global_device_ids=true | all-gather | bytes 36864 | tf_op jit(solution)/shard_map/all_gather | solution.py:18
  58.1 4.7 %multiply_bitcast_fusion = f32[64,8,32,128]{3,1,2,0:T(8,128)} fusion(f32[512,4096]{1,0:T(8,128)S(1)} %get-tuple-element.6, f32[512]{0:T(512)S(1)} %exponential_divide_fusion, f32[512]{0:T(512)S(1)} %get-tuple-element.5, f32[512]{0:T(512)S(1)} %copy-done.1), kind=kLoop, calls=%fused_computation.1 | loop fusion | flops 6291456 | bytes 16783360
  62.8 8.4 %copy.25 = f32[64,8,32,128]{3,2,1,0:T(8,128)} copy(f32[64,8,32,128]{3,1,2,0:T(8,128)} %multiply_bitcast_fusion) | data formatting | bytes 16777216
  71.3 10.4 %copy.18 = f32[512,32,128]{0,1,2:T(8,128)} copy(f32[512,32,128]{2,1,0:T(8,128)} %bitcast.36) | data formatting | bytes 16777216 | tf_op jit(solution)/shard_map/reshape.2
  81.7 7.2 %fusion.7 = f32[512,32,128]{0,1,2:T(8,128)} fusion(f32[512,32,128]{0,1,2:T(8,128)} %copy.18), kind=kOutput, calls=%fused_computation.27 | output fusion | flops 266338304 | bytes 16777216 | tf_op jit(solution)/shard_map/reduce-window
  88.9 0.8 slice_bitcast_fusion
  89.7 0.1 reduce-window.9
  89.8 4.4 %broadcast_add_fusion.2 = f32[512,32,128]{0,1,2:T(8,128)S(1)} fusion(f32[512,32,128]{0,1,2:T(8,128)} %fusion.7, f32[512,32]{0,1:T(8,128)S(1)} %slice.26), kind=kLoop, calls=%fused_computation.7 | loop fusion | flops 2097152 | bytes 16842752 | tf_op jit(solution)/shard_map/reduce_window_sum
  94.3 0.0 copy-start
  94.3 3.4 %copy-done = f32[512,32,128]{0,1,2:T(8,128)} copy-done((f32[512,32,128]{0,1,2:T(8,128)}, f32[512,32,128]{0,1,2:T(8,128)S(1)}, u32[]{:S(2)}) %copy-start) | copy-done | bytes 8388632
  97.7 8.1 %copy.20 = f32[512,32,128]{0,2,1:T(8,128)} copy(f32[512,32,128]{0,1,2:T(8,128)S(1)} %broadcast_add_fusion.2) | data formatting | bytes 16777216 | tf_op jit(solution)/shard_map/reduce_window_sum
  105.8 10.9 %copy.19 = f32[512,32,128]{2,1,0:T(8,128)} copy(f32[512,32,128]{0,1,2:T(8,128)} %copy-done) | data formatting | bytes 16777216 | tf_op jit(solution)/shard_map/reduce_window_sum
  116.7 0.7 slice.27
  117.4 21.3 %all-gather.1 = f32[4096,1]{0,1:T(1,128)S(1)} all-gather(f32[512,1]{0,1:T(1,128)S(1)} %slice.27), channel_id=3, replica_groups=mesh['dp'=2,'vp'=8] {'vp'}, dimensions={0}, use_global_device_ids=true | all-gather | bytes 18432 | tf_op jit(solution)/shard_map/all_gather | solution.py:23
  138.7 0.5 broadcast.50
  139.2 0.7 reduce.4
  139.9 9.6 %reduce_window_sum.20 = f32[8,64,4096]{2,1,0:T(8,128)} reshape(f32[512,32,128]{2,1,0:T(8,128)} %copy.19) | data formatting | bytes 16777216 | tf_op jit(solution)/shard_map/reduce_window_sum
  149.5 0.1 select_reduce_fusion
  149.6 0.1 add.24
  149.7 8.1 %broadcast_add_fusion.1 = f32[8,64,4096]{2,1,0:T(8,128)} fusion(f32[8,64,4096]{2,1,0:T(8,128)} %reduce_window_sum.20, f32[8,64]{1,0:T(8,128)S(1)} %add.24), kind=kLoop, calls=%fused_computation.6 | loop fusion | flops 2097152 | bytes 16779264 | tf_op jit(solution)/shard_map/add | solution.py:26
  157.8 0.0 copy-start.2
  157.8 11.0 %all-to-all-start = ((f32[8,64,4096]{2,1,0:T(8,128)}), f32[8,64,4096]{2,1,0:T(8,128)}, u32[]{:S(2)}, u32[]{:S(2)}) async-start(f32[8,64,4096]{2,1,0:T(8,128)} %broadcast_add_fusion.1), calls=%async_computation | async-start | bytes 16777216 | tf_op jit(solution)/shard_map/all_to_all | solution.py:31
  168.8 0.0 copy-done.2
  168.8 7.7 %broadcast_add_fusion = f32[512,4096]{0,1:T(8,128)} fusion(f32[512]{0:T(512)S(1)} %select_reduce_fusion, f32[512,32,128]{0,2,1:T(8,128)} %copy.20), kind=kLoop, calls=%fused_computation.5 | loop fusion | flops 2097152 | bytes 16779264 | tf_op jit(solution)/shard_map/add | solution.py:26
  176.5 19.1 %gather_fusion = f32[512]{0:T(512)S(1)} fusion(f32[512,4096]{0,1:T(8,128)} %broadcast_add_fusion, s32[512]{0:T(512)S(1)} %bitcast.34), kind=kCustom, calls=%fused_computation | custom fusion | bytes 8192 | tf_op jit(solution)/shard_map/jit(take_along_axis)/gather | solution.py:29
  195.6 71.8 %psum.7 = f32[512]{0:T(512)} all-reduce(f32[512]{0:T(512)S(1)} %select_select_fusion), channel_id=1, replica_groups=mesh['dp'=2,'vp'=8] {'vp'}, use_global_device_ids=true, to_apply=%region_7.8 | all-reduce | flops 512 | bytes 4096 | tf_op jit(solution)/shard_map/psum | solution.py:30
  267.4 0.0 all-to-all-done
  267.4 7.8 %copy.24 = f32[8,8,8,4096]{3,2,0,1:T(8,128)} copy(f32[8,8,8,4096]{3,2,1,0:T(8,128)} %bitcast.11) | data formatting | bytes 16777216 | tf_op jit(solution)/shard_map/all_to_all | solution.py:31
  (12 shorter events, 0.1 us)
Async XLA Ops:
  0.6 36.6 %copy-start.1 = (f32[512]{0:T(512)S(1)}, f32[512]{0:T(512)}, u32[]{:S(2)}) copy-start(f32[512]{0:T(512)} %param.6) | copy-start | bytes 6148
  94.3 3.4 %copy-start = (f32[512,32,128]{0,1,2:T(8,128)}, f32[512,32,128]{0,1,2:T(8,128)S(1)}, u32[]{:S(2)}) copy-start(f32[512,32,128]{0,1,2:T(8,128)S(1)} %broadcast_add_fusion.2) | copy-start | bytes 25165828
  157.8 11.0 %copy-start.2 = (s32[512]{0:T(512)S(1)}, s32[512]{0:T(512)}, u32[]{:S(2)}) copy-start(s32[512]{0:T(512)} %param.7) | copy-start | bytes 6148
  157.8 109.6 %all-to-all-start = ((f32[8,64,4096]{2,1,0:T(8,128)}), f32[8,64,4096]{2,1,0:T(8,128)}, u32[]{:S(2)}, u32[]{:S(2)}) async-start(f32[8,64,4096]{2,1,0:T(8,128)} %broadcast_add_fusion.1), calls=%async_computation | async-start | bytes 16777216 | tf_op jit(solution)/shard_map/all_to_all | solution.py:31
where the time goes:
time: 278 us; the launch traced here: 275 us
  blocking collectives  112 us (40%)
  local copies, waits for them, and re-layouts  79.9 us (29%)
  matrix products  36.6 us (13%)
  other arithmetic  35 us (13%)
  starting transfers between devices  11 us (4%)
    psum x1, blocking collectives, local_step(): cdf_at_target = lax.psum(jnp.where(in_shard, picked, 0.0), 'vp')  71.8 us
    another operation x6, local copies, waits for them, and re-layouts  39.9 us
    dot_general x1, matrix products, local_step(): logits = jnp.dot(hidden, w_local, preferred_element_type=jnp.float32)  36.6 us
    all_gather x1, blocking collectives, local_step(): totals = lax.all_gather(local_cdf[:, -1], 'vp')  21.3 us
    gather x1, local copies, waits for them, and re-layouts, local_step(): jnp.take_along_axis(cdf_cols, jnp.clip(local_ids, 0, local_vocab - 1)[:,...  19.1 us
    all_gather x1, blocking collectives, local_step(): shard_stats = lax.all_gather(jnp.stack([local_max, local_sum]), 'vp')  19 us
    add x2, other arithmetic, local_step(): cdf_cols = local_cdf + offset[:, None]  15.8 us
    unnamed x8, local copies, waits for them, and re-layouts  11.8 us
  transfers between devices with their start and end apart: 1, of which 0 were waited for; matrix products, arithmetic and copies ran while one was open for 10% of the time, Pallas kernels for 0%

commit v1 on v0

v1 whole, which is shorter than its diff:
```python
import functools

import jax
import jax.numpy as jnp
from jax import lax
from jax.experimental import pallas as pl
from jax.experimental.pallas import tpu as pltpu
from jax.sharding import PartitionSpec as P

MESH = pl.DeviceIdType.MESH
F32 = jnp.float32
BF16 = jnp.bfloat16
TILE = 256
LANES = 128
GROUP = 4
PEERS = ((2, 0), (2, 1), (0, 1), (1, 0), (3, 0), (1, 1), (3, 1))
EARLY = 3


def kernel(chips, h_hbm, w_hbm, temp_hbm, ids_hbm, table, picked,
           h, w, z, land, temp_row, ids_row, temp, ids, peak, stat_out, stats, rows, cols, inv_s, top, carry, tri,
           h_sem, w_sem, row_sem, send_sem, recv_sem, stat_send, stat_recv):
    n = 2 * chips
    me = lax.axis_index("vp")
    x, c = me // 2, me % 2
    batch, depth = h_hbm.shape
    vocab = w_hbm.shape[1]
    tiles = vocab // TILE
    own = batch // n
    pair = 2 * own

    def peer(i):
        dx, dc = PEERS[i]
        return lax.rem(x + dx, chips) * 2 + lax.rem(c + dc, 2)

    def source(i):
        dx, dc = PEERS[i]
        return lax.rem(x + chips - dx, chips) * 2 + lax.rem(c + dc, 2)

    def chip_rows(j):
        return pl.multiple_of(lax.rem(x + 2 + j, chips) * pair, pair)

    def h_copy(j):
        r = chip_rows(j)
        return pltpu.make_async_copy(h_hbm.at[pl.ds(r, pair), :], h.at[pl.ds(r, pair), :], h_sem.at[j])

    def w_copy(t):
        col = pl.multiple_of(t * TILE, TILE)
        slot = lax.rem(t, 2)
        return pltpu.make_async_copy(w_hbm.at[:, pl.ds(col, TILE)], w.at[slot], w_sem.at[slot])

    def send(i, t):
        to = peer(i)
        r = pl.multiple_of(to * own, own)
        return pltpu.make_async_remote_copy(
            src_ref=z.at[t, pl.ds(r, own), :], dst_ref=land.at[i, t], send_sem=send_sem, recv_sem=recv_sem.at[i, t],
            device_id={"vp": to}, device_id_type=MESH)

    def send_stat(i):
        return pltpu.make_async_remote_copy(
            src_ref=stat_out, dst_ref=stats.at[me], send_sem=stat_send.at[i], recv_sem=stat_recv.at[i],
            device_id={"vp": peer(i)}, device_id_type=MESH)

    def recv_stat(i):
        return pltpu.make_async_remote_copy(
            src_ref=stat_out, dst_ref=stats.at[source(i)], send_sem=stat_send.at[i], recv_sem=stat_recv.at[i],
            device_id={"vp": peer(i)}, device_id_type=MESH)

    temp_copy = pltpu.make_async_copy(temp_hbm, temp_row, row_sem.at[0])
    ids_copy = pltpu.make_async_copy(ids_hbm, ids_row, row_sem.at[1])
    temp_copy.start()
    h_copy(0).start()
    w_copy(0).start()
    for j in range(1, chips):
        h_copy(j).start()
    ids_copy.start()

    barrier = pltpu.get_barrier_semaphore()
    for i in range(n - 1):
        pl.semaphore_signal(barrier, inc=1, device_id={"vp": peer(i)}, device_id_type=MESH)

    row_id = lax.broadcasted_iota(jnp.int32, (TILE, TILE), 0)
    col_id = lax.broadcasted_iota(jnp.int32, (TILE, TILE), 1)
    tri[...] = jnp.where(row_id <= col_id, 1.0, 0.0).astype(BF16)
    temp_copy.wait()
    temp[...] = jnp.broadcast_to(temp_row[...], (LANES, batch)).T

    def tile_rows(t, slot, r, size, first):
        acc = jnp.dot(h[pl.ds(r, size), :], w[slot], preferred_element_type=F32)
        by = temp[pl.ds(r, size), :]
        left, right = acc[:, :LANES] * by, acc[:, LANES:] * by
        z[t, pl.ds(r, size), :LANES] = left
        z[t, pl.ds(r, size), LANES:] = right
        best = jnp.maximum(left, right)
        if not first:
            best = jnp.maximum(best, peak[pl.ds(r, size), :])
        peak[pl.ds(r, size), :] = best

    h_copy(0).wait()
    w_copy(0).wait()
    w_copy(1).start()
    tile_rows(0, 0, chip_rows(0), pair, True)
    pl.semaphore_wait(barrier, n - 1)
    send(0, 0).start()
    send(1, 0).start()

    @pl.loop(1, chips)
    def _(j):
        h_copy(j).wait()
        tile_rows(0, 0, chip_rows(j), pair, True)

    send(2, 0).start()

    @pl.loop(1, tiles)
    def _(t):
        @pl.when(t + 1 < tiles)
        def _():
            w_copy(t + 1).start()
        w_copy(t).wait()
        tile_rows(t, lax.rem(t, 2), 0, batch, False)
        for i in range(EARLY):
            send(i, t).start()

    ids_copy.wait()
    ids[...] = jnp.broadcast_to(ids_row[...], (LANES, batch)).T
    lane = lax.broadcasted_iota(jnp.int32, (own, LANES), 1)

    @pl.loop(0, n)
    def _(b):
        rs = pl.ds(pl.multiple_of(b * own, own), own)
        most = jnp.broadcast_to(jnp.max(peak[rs, :], axis=1, keepdims=True), (own, LANES))
        target = ids[rs, :] - (me * vocab) - lane

        def add(t, sums):
            total, below = sums
            for half in range(2):
                e = jnp.exp(z[t, rs, half * LANES:(half + 1) * LANES] - most)
                total = total + e
                below = below + jnp.where(target >= t * TILE + half * LANES, e, 0.0)
            return total, below

        zero = jnp.zeros((own, LANES), F32)
        total, below = lax.fori_loop(0, tiles, add, (zero, zero))
        total = jnp.sum(total, axis=1, keepdims=True)
        below = jnp.sum(below, axis=1, keepdims=True)
        peak[rs, :] = jnp.where(lane == 0, most, jnp.where(lane == 1, total, below))

    flipped = peak[...].T
    stat_out[...] = flipped[:4, :]
    stats[me] = flipped[:4, :]
    for i in range(n - 1):
        send_stat(i).start()

    @pl.loop(0, tiles)
    def _(t):
        for i in range(EARLY, n - 1):
            send(i, t).start()

    for i in range(n - 1):
        recv_stat(i).wait_recv()

    most = stats[0, 0:1, :]
    for d in range(1, n):
        most = jnp.maximum(most, stats[d, 0:1, :])
    mass = jnp.zeros_like(most)
    below = jnp.zeros_like(most)
    for d in range(n):
        rows[8 + d:9 + d, :] = mass
        scale = jnp.exp(stats[d, 0:1, :] - most)
        mass = mass + stats[d, 1:2, :] * scale
        below = below + stats[d, 2:3, :] * scale
    rows[0:1, :] = most
    rows[1:2, :] = mass
    picked[...] = below / mass

    mine = rows[:, pl.ds(pl.multiple_of(x * pair, pair), pair)]
    cols[...] = jnp.concatenate([mine, jnp.zeros((LANES - 16, LANES), F32)], axis=0).T
    mine = cols[pl.ds(pl.multiple_of(c * own, own), own), :]
    top[...] = jnp.broadcast_to(mine[:, 0:1], (own, TILE))
    scale = 1.0 / jnp.broadcast_to(mine[:, 1:2], (own, TILE))
    inv_s[...] = scale
    for i in range(n):
        d = source(i) if i < n - 1 else me
        start = jnp.sum(jnp.where(lane == 8 + d, mine, 0.0), axis=1, keepdims=True)
        carry[i] = jnp.broadcast_to(start, (own, TILE)) * scale

    def finish(i, d, t, count, read):
        e = jnp.concatenate([jnp.exp(read(t + k) - top[...]) * inv_s[...] for k in range(count)], axis=0)
        hi = e.astype(BF16)
        rest = e - hi.astype(F32)
        mid = rest.astype(BF16)
        low = (rest - mid.astype(F32)).astype(BF16)
        run = jnp.dot(hi, tri[...], preferred_element_type=F32)
        run = run + jnp.dot(mid, tri[...], preferred_element_type=F32)
        run = run + jnp.dot(low, tri[...], preferred_element_type=F32)
        base = carry[i]
        for k in range(count):
            part = run[k * own:(k + 1) * own, :]
            col = pl.multiple_of(d * vocab + (t + k) * TILE, TILE)
            table[:, pl.ds(col, TILE)] = part + base
            base = base + jnp.broadcast_to(part[:, TILE - 1:], (own, TILE))
        carry[i] = base

    my_rows = pl.ds(pl.multiple_of(me * own, own), own)

    @pl.loop(0, tiles // GROUP)
    def _(g):
        finish(n - 1, me, g * GROUP, GROUP, lambda t: z[t, my_rows, :])

    def arrive(i, t, count):
        for k in range(count):
            pltpu.make_async_copy(land.at[i, t + k], land.at[i, t + k], recv_sem.at[i, t + k]).wait()

    def source_of(i):
        dx = jnp.int32(0)
        dc = jnp.int32(0)
        for k, (kx, kc) in enumerate(PEERS):
            dx = dx + jnp.where(i == k, kx, 0)
            dc = dc + jnp.where(i == k, kc, 0)
        return lax.rem(x + chips - dx, chips) * 2 + lax.rem(c + dc, 2)

    def step(i, t, count):
        arrive(i, t, count)
        finish(i, source_of(i), t, count, lambda u: land[i, u])

    groups = tiles // GROUP

    @pl.loop(0, EARLY * groups)
    def _(k):
        step(k // groups, lax.rem(k, groups) * GROUP, GROUP)

    late = n - 1 - EARLY

    @pl.loop(0, late * (groups - 1))
    def _(k):
        step(EARLY + lax.rem(k, late), (k // late) * GROUP, GROUP)

    @pl.loop(0, late * GROUP)
    def _(k):
        step(EARLY + lax.rem(k, late), tiles - GROUP + k // late, 1)

    pltpu.make_async_copy(land, land, send_sem).wait()
    for i in range(n - 1):
        send_stat(i).wait_send()


def solution(mesh):
    n = mesh.shape["vp"]
    chips = n // 2

    def local_step(hidden, w_local, inv_temp, target_ids):
        batch, depth = hidden.shape
        vocab = w_local.shape[1]
        tiles = vocab // TILE
        own = batch // n
        hbm = pl.BlockSpec(memory_space=pltpu.HBM)
        vmem = pl.BlockSpec(memory_space=pltpu.VMEM)
        dma = pltpu.SemaphoreType.DMA
        table, picked = pl.pallas_call(
            functools.partial(kernel, chips),
            out_shape=(pltpu.VMEM((own, n * vocab), F32), jax.ShapeDtypeStruct((1, batch), F32)),
            in_specs=[hbm] * 4,
            out_specs=(vmem, vmem),
            scratch_shapes=[
                pltpu.VMEM((batch, depth), BF16),
                pltpu.VMEM((2, depth, TILE), BF16),
                pltpu.VMEM((tiles, batch, TILE), F32),
                pltpu.VMEM((n - 1, tiles, own, TILE), F32),
                pltpu.VMEM((1, batch), F32),
                pltpu.VMEM((1, batch), jnp.int32),
                pltpu.VMEM((batch, LANES), F32),
                pltpu.VMEM((batch, LANES), jnp.int32),
                pltpu.VMEM((batch, LANES), F32),
                pltpu.VMEM((4, batch), F32),
                pltpu.VMEM((n, 4, batch), F32),
                pltpu.VMEM((16, batch), F32),
                pltpu.VMEM((LANES, LANES), F32),
                pltpu.VMEM((own, TILE), F32),
                pltpu.VMEM((own, TILE), F32),
                pltpu.VMEM((n, own, TILE), F32),
                pltpu.VMEM((TILE, TILE), BF16),
                dma((chips,)), dma((2,)), dma((2,)), dma, dma((n - 1, tiles)), dma((n - 1,)), dma((n - 1,)),
            ],
            compiler_params=pltpu.CompilerParams(
                collective_id=0, has_side_effects=True, vmem_limit_bytes=52 * 2**20),
        )(hidden, w_local, inv_temp.reshape(1, batch), target_ids.reshape(1, batch))
        return table, picked.reshape(batch)

    return jax.shard_map(
        local_step,
        mesh=mesh,
        in_specs=(P("dp", None), P(None, "vp"), P("dp"), P("dp")),
        out_specs=(P(("dp", "vp"), None), P("dp")),
        check_vma=False,
    )
```

time: 278 us -> 107 us (0.38)
  blocking collectives: 112 us -> 0 us
  Pallas kernels: 0 us -> 102 us
  local copies, waits for them, and re-layouts: 79.9 us -> 3.98 us
  matrix products: 36.6 us -> 0 us
  other arithmetic: 35 us -> 0 us
  starting transfers between devices: 11 us -> 0 us
    pallas_call x0 -> x1, Pallas kernels: none -> 102 us  [local_step(): pl.pallas_call(functools.partial(kernel, chips), out_shape=(pltpu.VMEM((o...]
    psum x1 -> x0, blocking collectives: 71.8 us -> none  [local_step(): cdf_at_target = lax.psum(jnp.where(in_shard, picked, 0.0), 'vp')]
    all_gather x2 -> x0, blocking collectives: 40.3 us -> none  [the longest x1 21.3 us: local_step(): totals = lax.all_gather(local_cdf[:, -1], 'vp')]
    another operation x6 -> x0, local copies, waits for them, and re-layouts: 39.9 us -> none
    dot_general x1 -> x0, matrix products: 36.6 us -> none  [local_step(): logits = jnp.dot(hidden, w_local, preferred_element_type=jnp.float32)]
    gather x1 -> x0, local copies, waits for them, and re-layouts: 19.1 us -> none  [local_step(): jnp.take_along_axis(cdf_cols, jnp.clip(local_ids, 0, local_vocab - 1)[:,...]
    add x2 -> x0, other arithmetic: 15.8 us -> none  [local_step(): cdf_cols = local_cdf + offset[:, None]]
    another operation x3 -> x0, other arithmetic: 11.7 us -> none
  transfers between devices with their start and end apart: 1 -> 0, of which waited for: 0 -> 0; matrix products, arithmetic and copies ran while one was open for 10% -> 0% of each run, Pallas kernels for 0% -> 0%
where the time goes in v1:
time: 107 us
  Pallas kernels  102 us (95%)
  local copies, waits for them, and re-layouts  3.98 us (4%)
    pallas_call x1, Pallas kernels, local_step(): pl.pallas_call(functools.partial(kernel, chips), out_shape=(pltpu.VMEM((o...  102 us
    unnamed x4, local copies, waits for them, and re-layouts  3.98 us

profile of v1, /device:TPU:113, one launch (start us, length us, event | category | flops | bytes accessed | tf_op | source)
XLA Modules:
  0.0 106.9 jit_solution(9275211414786724538)
XLA Ops:
  0.6 102.3 %shard_map.59 = (f32[64,32768]{1,0:T(8,128)S(1)}, f32[1,512]{1,0:T(1,128)}) custom-call(bf16[512,6144]{1,0:T(8,128)(2,1)} %h_hbm.1, bf16[6144,4096]{1,0:T(8,128)(2,1)} %w_hbm.1, f32[1,512]{1,0:T(1,128)} %bitcast.3, s32[1,512]{1,0:T(1,128)} %bitcast.4), custom_call_target="tpu_custom_call" | custom-call | tf_op jit(solution)/shard_map/pallas_call | solution.py:259
  102.9 0.0 copy-start
  102.9 3.4 %copy.8 = f32[64,32768]{1,0:T(8,128)} copy(f32[64,32768]{1,0:T(8,128)S(1)} %get-tuple-element.6) | data formatting | bytes 16777216
  106.3 0.0 copy-done
  106.3 0.6 copy.9
Async XLA Ops:
  102.9 3.4 %copy-start = (f32[1,512]{1,0:T(1,128)S(1)}, f32[1,512]{1,0:T(1,128)}, u32[]{:S(2)}) copy-start(f32[1,512]{1,0:T(1,128)} %get-tuple-element.5) | copy-start | bytes 6148

commit v2 on v1

v2 whole, which is shorter than its diff:
```python
import functools

import jax
import jax.numpy as jnp
from jax import lax
from jax.experimental import pallas as pl
from jax.experimental.pallas import tpu as pltpu
from jax.sharding import PartitionSpec as P

MESH = pl.DeviceIdType.MESH
F32 = jnp.float32
BF16 = jnp.bfloat16
TILE = 256
LANES = 128
GROUP = 4
PIECES = 4
PEERS = ((2, 0), (2, 1), (0, 1), (1, 0), (3, 0), (1, 1), (3, 1))
EARLY = 3
CHIP_ORDER = (2, 1, 3, 0)


def kernel(chips, h_hbm, w_hbm, temp_hbm, ids_hbm, table, picked,
           h, w, z, land, temp_row, ids_row, temp, ids, peak, stat_out, stats, pick, cols, inv_s, top, carry, tri,
           h_sem, w_sem, first_sem, row_sem, send_sem, recv_sem, stat_send, stat_recv, pick_send, pick_recv):
    n = 2 * chips
    me = lax.axis_index("vp")
    x, c = me // 2, me % 2
    batch, depth = h_hbm.shape
    vocab = w_hbm.shape[1]
    tiles = vocab // TILE
    own = batch // n
    pair = 2 * own
    piece = depth // PIECES

    def peer(i):
        dx, dc = PEERS[i]
        return lax.rem(x + dx, chips) * 2 + lax.rem(c + dc, 2)

    def source(i):
        dx, dc = PEERS[i]
        return lax.rem(x + chips - dx, chips) * 2 + lax.rem(c + dc, 2)

    def held(dx):
        return CHIP_ORDER.index(dx) * pair

    def peer_rows(i):
        dx, dc = PEERS[i]
        return pl.ds(pl.multiple_of(held(dx) + lax.rem(c + dc, 2) * own, own), own)

    def whole_rows(j):
        return pl.ds(pl.multiple_of(lax.rem(x + CHIP_ORDER[j], chips) * pair, pair), pair)

    def h_copy(j):
        return pltpu.make_async_copy(h_hbm.at[whole_rows(j), :], h.at[j * pair:(j + 1) * pair, :], h_sem.at[j])

    def turned(row):
        parts = [row[:, whole_rows(j)] for j in range(chips)]
        return jnp.broadcast_to(jnp.concatenate(parts, axis=1), (LANES, batch)).T

    def w_copy(t):
        col = pl.multiple_of(lax.rem(t, tiles) * TILE, TILE)
        slot = lax.rem(t, 2)
        return pltpu.make_async_copy(w_hbm.at[:, pl.ds(col, TILE)], w.at[slot], w_sem.at[slot])

    def first_copies(k):
        ks = slice(k * piece, (k + 1) * piece)
        return (pltpu.make_async_copy(w_hbm.at[ks, :LANES], w.at[0, ks, :LANES], first_sem.at[0, k]),
                pltpu.make_async_copy(h_hbm.at[whole_rows(0), ks], h.at[:pair, ks], first_sem.at[1, k]))

    second_copy = pltpu.make_async_copy(w_hbm.at[:, LANES:TILE], w.at[0, :, LANES:], w_sem.at[0])

    def remote(src, dst, send, recv, to):
        return pltpu.make_async_remote_copy(
            src_ref=src, dst_ref=dst, send_sem=send, recv_sem=recv, device_id={"vp": to}, device_id_type=MESH)

    def send(i, t):
        return remote(z.at[t, peer_rows(i), :], land.at[i, t], send_sem, recv_sem.at[i, t], peer(i))

    def send_half(i, half):
        ls = slice(half * LANES, (half + 1) * LANES)
        return remote(z.at[0, peer_rows(i), ls], land.at[i, 0, :, ls], send_sem, recv_sem.at[i, 0], peer(i))

    def send_stat(i):
        at = stat_out.at[CHIP_ORDER.index(PEERS[i][0])]
        return remote(at, stats.at[me], stat_send.at[i], stat_recv.at[i], peer(i))

    def recv_stat(i):
        return remote(stat_out.at[0], stats.at[source(i)], stat_send.at[i], stat_recv.at[i], peer(i))

    def send_pick(dx):
        to = lax.rem(x + dx, chips) * 2 + c
        return remote(pick.at[x], pick.at[x], pick_send.at[dx], pick_recv.at[dx], to)

    def recv_pick(dx):
        at = pick.at[lax.rem(x + chips - dx, chips)]
        return remote(at, at, pick_send.at[dx], pick_recv.at[dx], lax.rem(x + dx, chips) * 2 + c)

    barrier = pltpu.get_barrier_semaphore()
    for i in range(n - 1):
        pl.semaphore_signal(barrier, inc=1, device_id={"vp": peer(i)}, device_id_type=MESH)
    temp_copy = pltpu.make_async_copy(temp_hbm, temp_row, row_sem.at[0])
    ids_copy = pltpu.make_async_copy(ids_hbm, ids_row, row_sem.at[1])
    temp_copy.start()
    for k in range(PIECES):
        for copy in first_copies(k):
            copy.start()
    second_copy.start()
    for j in (1, 2):
        h_copy(j).start()
    temp_copy.wait()
    temp[...] = turned(temp_row)

    acc = jnp.zeros((pair, LANES), F32)
    for k in range(PIECES):
        for copy in first_copies(k):
            copy.wait()
        ks = slice(k * piece, (k + 1) * piece)
        acc = acc + jnp.dot(h[:pair, ks], w[0, ks, :LANES], preferred_element_type=F32)
    acc = acc * temp[:pair, :]
    z[0, :pair, :LANES] = acc
    peak[:pair, :] = acc
    pl.semaphore_wait(barrier, n - 1)
    for i in range(2):
        send_half(i, 0).start()
    w_copy(1).start()
    h_copy(3).start()
    ids_copy.start()
    second_copy.wait()
    acc = jnp.dot(h[:pair, :], w[0, :, LANES:], preferred_element_type=F32) * temp[:pair, :]
    z[0, :pair, LANES:] = acc
    peak[:pair, :] = jnp.maximum(peak[:pair, :], acc)
    for i in range(2):
        send_half(i, 1).start()

    def tile_rows(t, slot, rs):
        acc = jnp.dot(h[rs, :], w[slot], preferred_element_type=F32)
        by = temp[rs, :]
        left, right = acc[:, :LANES] * by, acc[:, LANES:] * by
        z[t, rs, :LANES] = left
        z[t, rs, LANES:] = right
        return jnp.maximum(left, right)

    h_copy(1).wait()
    h_copy(2).wait()
    near = pl.ds(pair, 2 * pair)
    peak[near, :] = tile_rows(0, 0, near)
    for i in range(EARLY, n - 1):
        send(i, 0).start()
    here = pl.ds(3 * pair, pair)
    peak[here, :] = jnp.full((pair, LANES), -jnp.inf, F32)
    h_copy(3).wait()

    @pl.loop(1, tiles)
    def _(t):
        w_copy(t + 1).start()
        w_copy(t).wait()
        best = tile_rows(t, lax.rem(t, 2), pl.ds(0, batch))
        for i in range(EARLY):
            send(i, t).start()
        peak[...] = jnp.maximum(peak[...], best)

    w_copy(tiles).wait()
    peak[here, :] = jnp.maximum(peak[here, :], tile_rows(0, 0, here))
    send(2, 0).start()

    ids_copy.wait()
    ids[...] = turned(ids_row)
    lane = lax.broadcasted_iota(jnp.int32, (own, LANES), 1)

    @pl.loop(0, n)
    def _(b):
        rs = pl.ds(pl.multiple_of(b * own, own), own)
        most = jnp.broadcast_to(jnp.max(peak[rs, :], axis=1, keepdims=True), (own, LANES))
        target = ids[rs, :] - (me * vocab) - lane

        def add(t, sums):
            total, below = sums
            for half in range(2):
                e = jnp.exp(z[t, rs, half * LANES:(half + 1) * LANES] - most)
                total = total + e
                below = below + jnp.where(target >= t * TILE + half * LANES, e, 0.0)
            return total, below

        zero = jnp.zeros((own, LANES), F32)
        total, below = lax.fori_loop(0, tiles, add, (zero, zero))
        total = jnp.sum(total, axis=1, keepdims=True)
        below = jnp.sum(below, axis=1, keepdims=True)
        peak[rs, :] = jnp.where(lane == 0, most, jnp.where(lane == 1, total, below))

    flipped = peak[...].T
    for j in range(chips):
        stat_out[j] = flipped[:4, j * pair:(j + 1) * pair]
    stats[me] = stat_out[CHIP_ORDER.index(0)]
    for i in range(n - 1):
        send_stat(i).start()

    def send_near(first, last):
        @pl.loop(first, last)
        def _(t):
            for i in range(EARLY, n - 1):
                send(i, t).start()

    send_near(1, tiles // 2)
    row_id = lax.broadcasted_iota(jnp.int32, (TILE, TILE), 0)
    col_id = lax.broadcasted_iota(jnp.int32, (TILE, TILE), 1)
    tri[...] = jnp.where(row_id <= col_id, 1.0, 0.0).astype(BF16)
    for i in range(n - 1):
        recv_stat(i).wait_recv()

    most = stats[0, 0:1, :]
    for d in range(1, n):
        most = jnp.maximum(most, stats[d, 0:1, :])
    mass = jnp.zeros_like(most)
    below = jnp.zeros_like(most)
    lower = []
    for d in range(n):
        lower.append(mass)
        scale = jnp.exp(stats[d, 0:1, :] - most)
        mass = mass + stats[d, 1:2, :] * scale
        below = below + stats[d, 2:3, :] * scale
    pick[x] = below / mass
    for dx in range(1, chips):
        send_pick(dx).start()
    send_near(tiles // 2, tiles)

    mine = jnp.concatenate(lower + [most, mass, jnp.zeros((LANES - n - 2, pair), F32)], axis=0)
    cols[...] = mine.T
    mine = cols[pl.ds(pl.multiple_of(c * own, own), own), :]
    top[...] = jnp.broadcast_to(mine[:, n:n + 1], (own, TILE))
    scale = 1.0 / jnp.broadcast_to(mine[:, n + 1:n + 2], (own, TILE))
    inv_s[...] = scale
    for i in range(n):
        d = source(i) if i < n - 1 else me
        start = jnp.sum(jnp.where(lane == d, mine, 0.0), axis=1, keepdims=True)
        carry[i] = jnp.broadcast_to(start, (own, TILE)) * scale

    def finish(i, d, t, count, read):
        e = jnp.concatenate([jnp.exp(read(t + k) - top[...]) * inv_s[...] for k in range(count)], axis=0)
        hi = e.astype(BF16)
        rest = e - hi.astype(F32)
        mid = rest.astype(BF16)
        low = (rest - mid.astype(F32)).astype(BF16)
        run = jnp.dot(hi, tri[...], preferred_element_type=F32)
        run = run + jnp.dot(mid, tri[...], preferred_element_type=F32)
        run = run + jnp.dot(low, tri[...], preferred_element_type=F32)
        base = carry[i]
        for k in range(count):
            part = run[k * own:(k + 1) * own, :]
            col = pl.multiple_of(d * vocab + (t + k) * TILE, TILE)
            table[:, pl.ds(col, TILE)] = part + base
            base = base + jnp.broadcast_to(part[:, TILE - 1:], (own, TILE))
        carry[i] = base

    my_rows = pl.ds(pl.multiple_of(held(0) + c * own, own), own)

    @pl.loop(0, tiles // GROUP)
    def _(g):
        finish(n - 1, me, g * GROUP, GROUP, lambda t: z[t, my_rows, :])

    def source_of(i):
        dx = jnp.int32(0)
        dc = jnp.int32(0)
        for k, (kx, kc) in enumerate(PEERS):
            dx = dx + jnp.where(i == k, kx, 0)
            dc = dc + jnp.where(i == k, kc, 0)
        return lax.rem(x + chips - dx, chips) * 2 + lax.rem(c + dc, 2)

    def step(i, t, count):
        for k in range(count):
            pltpu.make_async_copy(land.at[i, t + k], land.at[i, t + k], recv_sem.at[i, t + k]).wait()
        finish(i, source_of(i), t, count, lambda u: land[i, u])

    groups = tiles // GROUP

    @pl.loop(0, EARLY * groups)
    def _(k):
        step(k // groups, lax.rem(k, groups) * GROUP, GROUP)

    for dx in range(1, chips):
        recv_pick(dx).wait_recv()
    for j in range(chips):
        picked[:, j * pair:(j + 1) * pair] = pick[j]

    late = n - 1 - EARLY

    @pl.loop(0, late * (groups - 1))
    def _(k):
        step(EARLY + lax.rem(k, late), (k // late) * GROUP, GROUP)

    @pl.loop(0, late * GROUP)
    def _(k):
        step(EARLY + lax.rem(k, late), tiles - GROUP + k // late, 1)

    pltpu.make_async_copy(land, land, send_sem).wait()
    for i in range(n - 1):
        send_stat(i).wait_send()
    for dx in range(1, chips):
        send_pick(dx).wait_send()


def write_out(table, picked, table_hbm, picked_hbm, sem):
    rows = table.shape[0]
    parts = rows // 8
    copies = [pltpu.make_async_copy(picked, picked_hbm, sem.at[parts])]
    for k in range(parts):
        copies.append(pltpu.make_async_copy(table.at[pl.ds(k * 8, 8), :], table_hbm.at[pl.ds(k * 8, 8), :], sem.at[k]))
    for copy in copies:
        copy.start()
    for copy in copies:
        copy.wait()


def solution(mesh):
    n = mesh.shape["vp"]
    chips = n // 2

    def local_step(hidden, w_local, inv_temp, target_ids):
        batch, depth = hidden.shape
        vocab = w_local.shape[1]
        tiles = vocab // TILE
        own = batch // n
        hbm = pl.BlockSpec(memory_space=pltpu.HBM)
        vmem = pl.BlockSpec(memory_space=pltpu.VMEM)
        dma = pltpu.SemaphoreType.DMA
        table, picked = pl.pallas_call(
            functools.partial(kernel, chips),
            out_shape=(pltpu.VMEM((own, n * vocab), F32), pltpu.VMEM((1, batch), F32)),
            in_specs=[hbm] * 4,
            out_specs=(vmem, vmem),
            scratch_shapes=[
                pltpu.VMEM((batch, depth), BF16),
                pltpu.VMEM((2, depth, TILE), BF16),
                pltpu.VMEM((tiles, batch, TILE), F32),
                pltpu.VMEM((n - 1, tiles, own, TILE), F32),
                pltpu.VMEM((1, batch), F32),
                pltpu.VMEM((1, batch), jnp.int32),
                pltpu.VMEM((batch, LANES), F32),
                pltpu.VMEM((batch, LANES), jnp.int32),
                pltpu.VMEM((batch, LANES), F32),
                pltpu.VMEM((chips, 4, 2 * own), F32),
                pltpu.VMEM((n, 4, 2 * own), F32),
                pltpu.VMEM((chips, 1, 2 * own), F32),
                pltpu.VMEM((2 * own, LANES), F32),
                pltpu.VMEM((own, TILE), F32),
                pltpu.VMEM((own, TILE), F32),
                pltpu.VMEM((n, own, TILE), F32),
                pltpu.VMEM((TILE, TILE), BF16),
                dma((chips,)), dma((2,)), dma((2, PIECES)), dma((2,)), dma, dma((n - 1, tiles)), dma((n - 1,)),
                dma((n - 1,)), dma((chips,)), dma((chips,)),
            ],
            compiler_params=pltpu.CompilerParams(
                collective_id=0, has_side_effects=True, vmem_limit_bytes=52 * 2**20),
        )(hidden, w_local, inv_temp.reshape(1, batch), target_ids.reshape(1, batch))
        table, picked = pl.pallas_call(
            write_out,
            out_shape=(pltpu.HBM(table.shape, F32), pltpu.HBM(picked.shape, F32)),
            in_specs=[vmem] * 2,
            out_specs=(hbm, hbm),
            scratch_shapes=[dma((own // 8 + 1,))],
            compiler_params=pltpu.CompilerParams(vmem_limit_bytes=2**20),
        )(table, picked)
        return table, picked.reshape(batch)

    return jax.shard_map(
        local_step,
        mesh=mesh,
        in_specs=(P("dp", None), P(None, "vp"), P("dp"), P("dp")),
        out_specs=(P(("dp", "vp"), None), P("dp")),
        check_vma=False,
    )
```

time: 107 us -> 105 us (0.981)
  local copies, waits for them, and re-layouts: 3.98 us -> 0 us
  Pallas kernels: 102 us -> 104 us
    unnamed x4 -> x0, local copies, waits for them, and re-layouts: 3.98 us -> none
    pallas_call x0 -> x1, Pallas kernels: none -> 3.38 us  [local_step(): pl.pallas_call(write_out, out_shape=(pltpu.HBM(table.shape, F32), pltpu.H...]
    pallas_call x1, Pallas kernels: 102 us -> 101 us  [local_step(): pl.pallas_call(functools.partial(kernel, chips), out_shape=(pltpu.VMEM((o...]
where the time goes in v2:
time: 105 us
  Pallas kernels  104 us (99%)
    pallas_call x1, Pallas kernels, local_step(): pl.pallas_call(functools.partial(kernel, chips), out_shape=(pltpu.VMEM((o...  101 us
    pallas_call x1, Pallas kernels, local_step(): pl.pallas_call(write_out, out_shape=(pltpu.HBM(table.shape, F32), pltpu.H...  3.38 us

profile of v2, /device:TPU:113, one launch (start us, length us, event | category | flops | bytes accessed | tf_op | source)
XLA Modules:
  0.0 104.6 jit_solution(11822612131768449271)
XLA Ops:
  0.6 100.5 %shard_map.59 = (f32[64,32768]{1,0:T(8,128)S(1)}, f32[1,512]{1,0:T(1,128)S(1)}) custom-call(bf16[512,6144]{1,0:T(8,128)(2,1)} %h_hbm.1, bf16[6144,4096]{1,0:T(8,128)(2,1)} %w_hbm.1, f32[1,512]{1,0:T(1,128)} %bitcast.3, s32[1,512]{1,0:T(1,128)} %bitcast.4), custom_call_target="tpu_custom_call" | custom-call | tf_op jit(solution)/shard_map/pallas_call | solution.py:325
  101.2 3.4 %shard_map.60 = (f32[64,32768]{1,0:T(8,128)}, f32[1,512]{1,0:T(1,128)}) custom-call(f32[64,32768]{1,0:T(8,128)S(1)} %get-tuple-element.6.table, f32[1,512]{1,0:T(1,128)S(1)} %get-tuple-element.7.picked), custom_call_target="tpu_custom_call" | custom-call | tf_op jit(solution)/shard_map/pallas_call | solution.py:354

commit v3 on v2

--- a/solution.py
+++ b/solution.py
@@ -13,15 +13,15 @@
 TILE = 256
 LANES = 128
 GROUP = 4
+WAITS = (8, 4, 2, 1, 1)
 PIECES = 4
-PEERS = ((2, 0), (2, 1), (0, 1), (1, 0), (3, 0), (1, 1), (3, 1))
-EARLY = 3
+PEERS = ((2, 0), (2, 1), (1, 0), (3, 0), (1, 1), (3, 1), (0, 1))
 CHIP_ORDER = (2, 1, 3, 0)
 
 
 def kernel(chips, h_hbm, w_hbm, temp_hbm, ids_hbm, table, picked,
            h, w, z, land, temp_row, ids_row, temp, ids, peak, stat_out, stats, pick, cols, inv_s, top, carry, tri,
-           h_sem, w_sem, first_sem, row_sem, send_sem, recv_sem, stat_send, stat_recv, pick_send, pick_recv):
+           h_sem, w_sem, first_sem, row_sem, send_sem, recv_sem, near_sem, stat_send, stat_recv, pick_send, pick_recv):
     n = 2 * chips
     me = lax.axis_index("vp")
     x, c = me // 2, me % 2
@@ -31,6 +31,8 @@
     own = batch // n
     pair = 2 * own
     piece = depth // PIECES
+    remote_peers = n - 2
+    firsts = [sum(WAITS[:k]) for k in range(len(WAITS))]
 
     def peer(i):
         dx, dc = PEERS[i]
@@ -73,27 +75,36 @@
         return pltpu.make_async_remote_copy(
             src_ref=src, dst_ref=dst, send_sem=send, recv_sem=recv, device_id={"vp": to}, device_id_type=MESH)
 
+    def counter(t):
+        k = 0
+        for first in firsts[1:]:
+            k = k + jnp.where(t >= first, 1, 0)
+        return k
+
+    def arrival(i, t):
+        return near_sem if i == remote_peers else recv_sem.at[i, counter(t)]
+
     def send(i, t):
-        return remote(z.at[t, peer_rows(i), :], land.at[i, t], send_sem, recv_sem.at[i, t], peer(i))
+        return remote(z.at[t, peer_rows(i), :], land.at[i, t], send_sem, arrival(i, t), peer(i))
+
+    def send_tile(t):
+        for i in range(remote_peers):
+            send(i, t).start()
 
     def send_half(i, half):
         ls = slice(half * LANES, (half + 1) * LANES)
-        return remote(z.at[0, peer_rows(i), ls], land.at[i, 0, :, ls], send_sem, recv_sem.at[i, 0], peer(i))
+        return remote(z.at[0, peer_rows(i), ls], land.at[i, 0, :, ls], send_sem, arrival(i, 0), peer(i))
 
     def send_stat(i):
         at = stat_out.at[CHIP_ORDER.index(PEERS[i][0])]
-        return remote(at, stats.at[me], stat_send.at[i], stat_recv.at[i], peer(i))
-
-    def recv_stat(i):
-        return remote(stat_out.at[0], stats.at[source(i)], stat_send.at[i], stat_recv.at[i], peer(i))
+        return remote(at, stats.at[me], stat_send, stat_recv, peer(i))
 
     def send_pick(dx):
         to = lax.rem(x + dx, chips) * 2 + c
-        return remote(pick.at[x], pick.at[x], pick_send.at[dx], pick_recv.at[dx], to)
-
-    def recv_pick(dx):
-        at = pick.at[lax.rem(x + chips - dx, chips)]
-        return remote(at, at, pick_send.at[dx], pick_recv.at[dx], lax.rem(x + dx, chips) * 2 + c)
+        return remote(pick.at[x], pick.at[x], pick_send, pick_recv, to)
+
+    def counted(ref, sem):
+        pltpu.make_async_copy(ref, ref, sem).wait()
 
     barrier = pltpu.get_barrier_semaphore()
     for i in range(n - 1):
@@ -144,7 +155,7 @@
     h_copy(2).wait()
     near = pl.ds(pair, 2 * pair)
     peak[near, :] = tile_rows(0, 0, near)
-    for i in range(EARLY, n - 1):
+    for i in range(2, remote_peers):
         send(i, 0).start()
     here = pl.ds(3 * pair, pair)
     peak[here, :] = jnp.full((pair, LANES), -jnp.inf, F32)
@@ -155,13 +166,16 @@
         w_copy(t + 1).start()
         w_copy(t).wait()
         best = tile_rows(t, lax.rem(t, 2), pl.ds(0, batch))
-        for i in range(EARLY):
-            send(i, t).start()
+        send(remote_peers, t).start()
+
+        @pl.when(lax.rem(t, 2) == 1)
+        def _():
+            send_tile((t + 1) // 2)
         peak[...] = jnp.maximum(peak[...], best)
 
     w_copy(tiles).wait()
     peak[here, :] = jnp.maximum(peak[here, :], tile_rows(0, 0, here))
-    send(2, 0).start()
+    send(remote_peers, 0).start()
 
     ids_copy.wait()
     ids[...] = turned(ids_row)
@@ -194,18 +208,12 @@
     for i in range(n - 1):
         send_stat(i).start()
 
-    def send_near(first, last):
-        @pl.loop(first, last)
-        def _(t):
-            for i in range(EARLY, n - 1):
-                send(i, t).start()
-
-    send_near(1, tiles // 2)
+    sent = tiles // 2 + 1
+    pl.loop(sent, sent + 3)(send_tile)
     row_id = lax.broadcasted_iota(jnp.int32, (TILE, TILE), 0)
     col_id = lax.broadcasted_iota(jnp.int32, (TILE, TILE), 1)
     tri[...] = jnp.where(row_id <= col_id, 1.0, 0.0).astype(BF16)
-    for i in range(n - 1):
-        recv_stat(i).wait_recv()
+    counted(stats.at[pl.ds(0, n - 1)], stat_recv)
 
     most = stats[0, 0:1, :]
     for d in range(1, n):
@@ -221,7 +229,7 @@
     pick[x] = below / mass
     for dx in range(1, chips):
         send_pick(dx).start()
-    send_near(tiles // 2, tiles)
+    pl.loop(sent + 3, tiles)(send_tile)
 
     mine = jnp.concatenate(lower + [most, mass, jnp.zeros((LANES - n - 2, pair), F32)], axis=0)
     cols[...] = mine.T
@@ -266,36 +274,35 @@
         return lax.rem(x + chips - dx, chips) * 2 + lax.rem(c + dc, 2)
 
     def step(i, t, count):
-        for k in range(count):
-            pltpu.make_async_copy(land.at[i, t + k], land.at[i, t + k], recv_sem.at[i, t + k]).wait()
         finish(i, source_of(i), t, count, lambda u: land[i, u])
 
-    groups = tiles // GROUP
-
-    @pl.loop(0, EARLY * groups)
+    counted(land.at[remote_peers], near_sem)
+
+    @pl.loop(0, tiles // GROUP)
     def _(k):
-        step(k // groups, lax.rem(k, groups) * GROUP, GROUP)
-
-    for dx in range(1, chips):
-        recv_pick(dx).wait_recv()
-    for j in range(chips):
-        picked[:, j * pair:(j + 1) * pair] = pick[j]
-
-    late = n - 1 - EARLY
-
-    @pl.loop(0, late * (groups - 1))
-    def _(k):
-        step(EARLY + lax.rem(k, late), (k // late) * GROUP, GROUP)
-
-    @pl.loop(0, late * GROUP)
-    def _(k):
-        step(EARLY + lax.rem(k, late), tiles - GROUP + k // late, 1)
-
-    pltpu.make_async_copy(land, land, send_sem).wait()
-    for i in range(n - 1):
-        send_stat(i).wait_send()
-    for dx in range(1, chips):
-        send_pick(dx).wait_send()
+        step(remote_peers, k * GROUP, GROUP)
+
+    for k, (first, size) in enumerate(zip(firsts, WAITS)):
+        if k == len(WAITS) - 1:
+            counted(pick.at[pl.ds(0, chips - 1)], pick_recv)
+            for j in range(chips):
+                picked[:, j * pair:(j + 1) * pair] = pick[j]
+        count = min(size, GROUP)
+        parts = size // count
+
+        @pl.loop(0, remote_peers * parts)
+        def _(u):
+            i = lax.rem(u, remote_peers)
+            part = u // remote_peers
+
+            @pl.when(part == 0)
+            def _():
+                counted(land.at[i, pl.ds(first, size)], recv_sem.at[i, k])
+            step(i, first + part * count, count)
+
+    counted(land, send_sem)
+    counted(stats.at[pl.ds(0, n - 1)], stat_send)
+    counted(pick.at[pl.ds(0, chips - 1)], pick_send)
 
 
 def write_out(table, picked, table_hbm, picked_hbm, sem):
@@ -345,8 +352,8 @@
                 pltpu.VMEM((own, TILE), F32),
                 pltpu.VMEM((n, own, TILE), F32),
                 pltpu.VMEM((TILE, TILE), BF16),
-                dma((chips,)), dma((2,)), dma((2, PIECES)), dma((2,)), dma, dma((n - 1, tiles)), dma((n - 1,)),
-                dma((n - 1,)), dma((chips,)), dma((chips,)),
+                dma((chips,)), dma((2,)), dma((2, PIECES)), dma((2,)), dma, dma((n - 2, len(WAITS))), dma,
+                dma, dma, dma, dma,
             ],
             compiler_params=pltpu.CompilerParams(
                 collective_id=0, has_side_effects=True, vmem_limit_bytes=52 * 2**20),

time: 105 us -> 104 us (level)
  no operation moved by 1% of the time
where the time goes in v3:
time: 104 us
  Pallas kernels  103 us (99%)
    pallas_call x1, Pallas kernels, local_step(): pl.pallas_call(functools.partial(kernel, chips), out_shape=(pltpu.VMEM((o...  99.5 us
    pallas_call x1, Pallas kernels, local_step(): pl.pallas_call(write_out, out_shape=(pltpu.HBM(table.shape, F32), pltpu.H...  3.38 us

profile of v3, /device:TPU:113, one launch (start us, length us, event | category | flops | bytes accessed | tf_op | source)
XLA Modules:
  0.0 103.5 jit_solution(3082522250241938048)
XLA Ops:
  0.6 99.5 %shard_map.59 = (f32[64,32768]{1,0:T(8,128)S(1)}, f32[1,512]{1,0:T(1,128)S(1)}) custom-call(bf16[512,6144]{1,0:T(8,128)(2,1)} %h_hbm.1, bf16[6144,4096]{1,0:T(8,128)(2,1)} %w_hbm.1, f32[1,512]{1,0:T(1,128)} %bitcast.3, s32[1,512]{1,0:T(1,128)} %bitcast.4), custom_call_target="tpu_custom_call" | custom-call | tf_op jit(solution)/shard_map/pallas_call | solution.py:332
  100.1 3.4 %shard_map.60 = (f32[64,32768]{1,0:T(8,128)}, f32[1,512]{1,0:T(1,128)}) custom-call(f32[64,32768]{1,0:T(8,128)S(1)} %get-tuple-element.6.table, f32[1,512]{1,0:T(1,128)S(1)} %get-tuple-element.7.picked), custom_call_target="tpu_custom_call" | custom-call | tf_op jit(solution)/shard_map/pallas_call | solution.py:361

commit v4 on v3

--- a/solution.py
+++ b/solution.py
@@ -13,15 +13,40 @@
 TILE = 256
 LANES = 128
 GROUP = 4
-WAITS = (8, 4, 2, 1, 1)
-PIECES = 4
+WAITS = (8, 7, 1)
 PEERS = ((2, 0), (2, 1), (1, 0), (3, 0), (1, 1), (3, 1), (0, 1))
 CHIP_ORDER = (2, 1, 3, 0)
 
 
-def kernel(chips, h_hbm, w_hbm, temp_hbm, ids_hbm, table, picked,
-           h, w, z, land, temp_row, ids_row, temp, ids, peak, stat_out, stats, pick, cols, inv_s, top, carry, tri,
-           h_sem, w_sem, first_sem, row_sem, send_sem, recv_sem, near_sem, stat_send, stat_recv, pick_send, pick_recv):
+def peer_of(chips, x, c, i):
+    dx, dc = PEERS[i]
+    return lax.rem(x + dx, chips) * 2 + lax.rem(c + dc, 2)
+
+
+def source_of(chips, x, c, i):
+    dx, dc = PEERS[i]
+    return lax.rem(x + chips - dx, chips) * 2 + lax.rem(c + dc, 2)
+
+
+def triangle():
+    row_id = lax.broadcasted_iota(jnp.int32, (TILE, TILE), 0)
+    col_id = lax.broadcasted_iota(jnp.int32, (TILE, TILE), 1)
+    return jnp.where(row_id <= col_id, 1.0, 0.0).astype(BF16)
+
+
+def running_sum(e, tri):
+    hi = e.astype(BF16)
+    rest = e - hi.astype(F32)
+    mid = rest.astype(BF16)
+    low = (rest - mid.astype(F32)).astype(BF16)
+    run = jnp.dot(hi, tri, preferred_element_type=F32)
+    run = run + jnp.dot(mid, tri, preferred_element_type=F32)
+    return run + jnp.dot(low, tri, preferred_element_type=F32)
+
+
+def kernel(chips, h_hbm, w_hbm, temp_hbm, ids_hbm, table, picked, last, top, inv_s, carry,
+           h, w, z, land, temp_row, ids_row, temp, ids, peak, stat_out, stats, pick, cols, tri,
+           h_sem, w_sem, row_sem, send_sem, recv_sem, near_sem, stat_send, stat_recv, pick_send, pick_recv):
     n = 2 * chips
     me = lax.axis_index("vp")
     x, c = me // 2, me % 2
@@ -30,17 +55,14 @@
     tiles = vocab // TILE
     own = batch // n
     pair = 2 * own
-    piece = depth // PIECES
     remote_peers = n - 2
     firsts = [sum(WAITS[:k]) for k in range(len(WAITS))]
 
     def peer(i):
-        dx, dc = PEERS[i]
-        return lax.rem(x + dx, chips) * 2 + lax.rem(c + dc, 2)
+        return peer_of(chips, x, c, i)
 
     def source(i):
-        dx, dc = PEERS[i]
-        return lax.rem(x + chips - dx, chips) * 2 + lax.rem(c + dc, 2)
+        return source_of(chips, x, c, i)
 
     def held(dx):
         return CHIP_ORDER.index(dx) * pair
@@ -64,12 +86,9 @@
         slot = lax.rem(t, 2)
         return pltpu.make_async_copy(w_hbm.at[:, pl.ds(col, TILE)], w.at[slot], w_sem.at[slot])
 
-    def first_copies(k):
-        ks = slice(k * piece, (k + 1) * piece)
-        return (pltpu.make_async_copy(w_hbm.at[ks, :LANES], w.at[0, ks, :LANES], first_sem.at[0, k]),
-                pltpu.make_async_copy(h_hbm.at[whole_rows(0), ks], h.at[:pair, ks], first_sem.at[1, k]))
-
-    second_copy = pltpu.make_async_copy(w_hbm.at[:, LANES:TILE], w.at[0, :, LANES:], w_sem.at[0])
+    first_w = pltpu.make_async_copy(w_hbm.at[:, :LANES], w.at[0, :, :LANES], w_sem.at[1])
+    first_h = h_copy(0)
+    second_w = pltpu.make_async_copy(w_hbm.at[:, LANES:TILE], w.at[0, :, LANES:], w_sem.at[0])
 
     def remote(src, dst, send, recv, to):
         return pltpu.make_async_remote_copy(
@@ -87,6 +106,9 @@
     def send(i, t):
         return remote(z.at[t, peer_rows(i), :], land.at[i, t], send_sem, arrival(i, t), peer(i))
 
+    def send_last(i):
+        return remote(z.at[tiles - 1, peer_rows(i), :], last.at[i], send_sem, arrival(i, tiles - 1), peer(i))
+
     def send_tile(t):
         for i in range(remote_peers):
             send(i, t).start()
@@ -106,28 +128,23 @@
     def counted(ref, sem):
         pltpu.make_async_copy(ref, ref, sem).wait()
 
+    temp_copy = pltpu.make_async_copy(temp_hbm, temp_row, row_sem.at[0])
+    ids_copy = pltpu.make_async_copy(ids_hbm, ids_row, row_sem.at[1])
+    first_w.start()
+    first_h.start()
+    temp_copy.start()
     barrier = pltpu.get_barrier_semaphore()
     for i in range(n - 1):
         pl.semaphore_signal(barrier, inc=1, device_id={"vp": peer(i)}, device_id_type=MESH)
-    temp_copy = pltpu.make_async_copy(temp_hbm, temp_row, row_sem.at[0])
-    ids_copy = pltpu.make_async_copy(ids_hbm, ids_row, row_sem.at[1])
-    temp_copy.start()
-    for k in range(PIECES):
-        for copy in first_copies(k):
-            copy.start()
-    second_copy.start()
+    second_w.start()
     for j in (1, 2):
         h_copy(j).start()
     temp_copy.wait()
     temp[...] = turned(temp_row)
 
-    acc = jnp.zeros((pair, LANES), F32)
-    for k in range(PIECES):
-        for copy in first_copies(k):
-            copy.wait()
-        ks = slice(k * piece, (k + 1) * piece)
-        acc = acc + jnp.dot(h[:pair, ks], w[0, ks, :LANES], preferred_element_type=F32)
-    acc = acc * temp[:pair, :]
+    first_w.wait()
+    first_h.wait()
+    acc = jnp.dot(h[:pair, :], w[0, :, :LANES], preferred_element_type=F32) * temp[:pair, :]
     z[0, :pair, :LANES] = acc
     peak[:pair, :] = acc
     pl.semaphore_wait(barrier, n - 1)
@@ -136,7 +153,7 @@
     w_copy(1).start()
     h_copy(3).start()
     ids_copy.start()
-    second_copy.wait()
+    second_w.wait()
     acc = jnp.dot(h[:pair, :], w[0, :, LANES:], preferred_element_type=F32) * temp[:pair, :]
     z[0, :pair, LANES:] = acc
     peak[:pair, :] = jnp.maximum(peak[:pair, :], acc)
@@ -210,9 +227,7 @@
 
     sent = tiles // 2 + 1
     pl.loop(sent, sent + 3)(send_tile)
-    row_id = lax.broadcasted_iota(jnp.int32, (TILE, TILE), 0)
-    col_id = lax.broadcasted_iota(jnp.int32, (TILE, TILE), 1)
-    tri[...] = jnp.where(row_id <= col_id, 1.0, 0.0).astype(BF16)
+    tri[...] = triangle()
     counted(stats.at[pl.ds(0, n - 1)], stat_recv)
 
     most = stats[0, 0:1, :]
@@ -229,7 +244,9 @@
     pick[x] = below / mass
     for dx in range(1, chips):
         send_pick(dx).start()
-    pl.loop(sent + 3, tiles)(send_tile)
+    pl.loop(sent + 3, tiles - 1)(send_tile)
+    for i in range(remote_peers):
+        send_last(i).start()
 
     mine = jnp.concatenate(lower + [most, mass, jnp.zeros((LANES - n - 2, pair), F32)], axis=0)
     cols[...] = mine.T
@@ -244,13 +261,7 @@
 
     def finish(i, d, t, count, read):
         e = jnp.concatenate([jnp.exp(read(t + k) - top[...]) * inv_s[...] for k in range(count)], axis=0)
-        hi = e.astype(BF16)
-        rest = e - hi.astype(F32)
-        mid = rest.astype(BF16)
-        low = (rest - mid.astype(F32)).astype(BF16)
-        run = jnp.dot(hi, tri[...], preferred_element_type=F32)
-        run = run + jnp.dot(mid, tri[...], preferred_element_type=F32)
-        run = run + jnp.dot(low, tri[...], preferred_element_type=F32)
+        run = running_sum(e, tri[...])
         base = carry[i]
         for k in range(count):
             part = run[k * own:(k + 1) * own, :]
@@ -265,16 +276,14 @@
     def _(g):
         finish(n - 1, me, g * GROUP, GROUP, lambda t: z[t, my_rows, :])
 
-    def source_of(i):
-        dx = jnp.int32(0)
-        dc = jnp.int32(0)
-        for k, (kx, kc) in enumerate(PEERS):
-            dx = dx + jnp.where(i == k, kx, 0)
-            dc = dc + jnp.where(i == k, kc, 0)
-        return lax.rem(x + chips - dx, chips) * 2 + lax.rem(c + dc, 2)
+    def source_at(i):
+        d = jnp.int32(0)
+        for k in range(n - 1):
+            d = d + jnp.where(i == k, source(k), 0)
+        return d
 
     def step(i, t, count):
-        finish(i, source_of(i), t, count, lambda u: land[i, u])
+        finish(i, source_at(i), t, count, lambda u: land[i, u])
 
     counted(land.at[remote_peers], near_sem)
 
@@ -282,12 +291,9 @@
     def _(k):
         step(remote_peers, k * GROUP, GROUP)
 
-    for k, (first, size) in enumerate(zip(firsts, WAITS)):
-        if k == len(WAITS) - 1:
-            counted(pick.at[pl.ds(0, chips - 1)], pick_recv)
-            for j in range(chips):
-                picked[:, j * pair:(j + 1) * pair] = pick[j]
-        count = min(size, GROUP)
+    for k in range(len(WAITS) - 1):
+        first, size = firsts[k], WAITS[k]
+        count = min(size, 2 * GROUP - 1) if size % GROUP else GROUP
         parts = size // count
 
         @pl.loop(0, remote_peers * parts)
@@ -300,21 +306,43 @@
                 counted(land.at[i, pl.ds(first, size)], recv_sem.at[i, k])
             step(i, first + part * count, count)
 
+    counted(pick.at[pl.ds(0, chips - 1)], pick_recv)
+    for j in range(chips):
+        picked[:, j * pair:(j + 1) * pair] = pick[j]
+    for i in range(remote_peers):
+        counted(last.at[i], recv_sem.at[i, len(WAITS) - 1])
     counted(land, send_sem)
     counted(stats.at[pl.ds(0, n - 1)], stat_send)
     counted(pick.at[pl.ds(0, chips - 1)], pick_send)
 
 
-def write_out(table, picked, table_hbm, picked_hbm, sem):
-    rows = table.shape[0]
-    parts = rows // 8
-    copies = [pltpu.make_async_copy(picked, picked_hbm, sem.at[parts])]
-    for k in range(parts):
-        copies.append(pltpu.make_async_copy(table.at[pl.ds(k * 8, 8), :], table_hbm.at[pl.ds(k * 8, 8), :], sem.at[k]))
-    for copy in copies:
-        copy.start()
-    for copy in copies:
-        copy.wait()
+def write_out(chips, table, picked, last, top, inv_s, carry, table_hbm, picked_hbm, done, sem):
+    n = 2 * chips
+    me = lax.axis_index("vp")
+    x, c = me // 2, me % 2
+    own, width = table.shape
+    vocab = width // n
+    bulk = vocab - TILE
+
+    def put(d, first, size, sem, source=None):
+        cs = pl.ds(pl.multiple_of(d * vocab + first, TILE), size)
+        return pltpu.make_async_copy(table.at[:, cs] if source is None else source, table_hbm.at[:, cs], sem)
+
+    for d in range(n):
+        put(d, 0, bulk, sem.at[0]).start()
+    for d in (me, source_of(chips, x, c, n - 2)):
+        put(d, bulk, TILE, sem.at[1]).start()
+    picked_copy = pltpu.make_async_copy(picked, picked_hbm, sem.at[2])
+    picked_copy.start()
+    e = jnp.concatenate([jnp.exp(last[i] - top[...]) * inv_s[...] for i in range(n - 2)], axis=0)
+    run = running_sum(e, triangle())
+    for i in range(n - 2):
+        done[i] = run[i * own:(i + 1) * own, :] + carry[i]
+    for i in range(n - 2):
+        put(source_of(chips, x, c, i), bulk, TILE, sem.at[1], done.at[i]).start()
+    picked_copy.wait()
+    put(0, 0, n * bulk, sem.at[0]).wait()
+    put(0, 0, n * TILE, sem.at[1]).wait()
 
 
 def solution(mesh):
@@ -329,11 +357,13 @@
         hbm = pl.BlockSpec(memory_space=pltpu.HBM)
         vmem = pl.BlockSpec(memory_space=pltpu.VMEM)
         dma = pltpu.SemaphoreType.DMA
-        table, picked = pl.pallas_call(
+        out = (pltpu.VMEM((own, n * vocab), F32), pltpu.VMEM((1, batch), F32), pltpu.VMEM((n - 2, own, TILE), F32),
+               pltpu.VMEM((own, TILE), F32), pltpu.VMEM((own, TILE), F32), pltpu.VMEM((n, own, TILE), F32))
+        parts = pl.pallas_call(
             functools.partial(kernel, chips),
-            out_shape=(pltpu.VMEM((own, n * vocab), F32), pltpu.VMEM((1, batch), F32)),
+            out_shape=out,
             in_specs=[hbm] * 4,
-            out_specs=(vmem, vmem),
+            out_specs=(vmem,) * len(out),
             scratch_shapes=[
                 pltpu.VMEM((batch, depth), BF16),
                 pltpu.VMEM((2, depth, TILE), BF16),
@@ -348,24 +378,21 @@
                 pltpu.VMEM((n, 4, 2 * own), F32),
                 pltpu.VMEM((chips, 1, 2 * own), F32),
                 pltpu.VMEM((2 * own, LANES), F32),
-                pltpu.VMEM((own, TILE), F32),
-                pltpu.VMEM((own, TILE), F32),
-                pltpu.VMEM((n, own, TILE), F32),
                 pltpu.VMEM((TILE, TILE), BF16),
-                dma((chips,)), dma((2,)), dma((2, PIECES)), dma((2,)), dma, dma((n - 2, len(WAITS))), dma,
+                dma((chips,)), dma((2,)), dma((2,)), dma, dma((n - 2, len(WAITS))), dma,
                 dma, dma, dma, dma,
             ],
             compiler_params=pltpu.CompilerParams(
                 collective_id=0, has_side_effects=True, vmem_limit_bytes=52 * 2**20),
         )(hidden, w_local, inv_temp.reshape(1, batch), target_ids.reshape(1, batch))
         table, picked = pl.pallas_call(
-            write_out,
-            out_shape=(pltpu.HBM(table.shape, F32), pltpu.HBM(picked.shape, F32)),
-            in_specs=[vmem] * 2,
+            functools.partial(write_out, chips),
+            out_shape=(pltpu.HBM((own, n * vocab), F32), pltpu.HBM((1, batch), F32)),
+            in_specs=[vmem] * len(out),
             out_specs=(hbm, hbm),
-            scratch_shapes=[dma((own // 8 + 1,))],
-            compiler_params=pltpu.CompilerParams(vmem_limit_bytes=2**20),
-        )(table, picked)
+            scratch_shapes=[pltpu.VMEM((n - 2, own, TILE), F32), dma((3,))],
+            compiler_params=pltpu.CompilerParams(vmem_limit_bytes=8 * 2**20),
+        )(*parts)
         return table, picked.reshape(batch)
 
     return jax.shard_map(

time: 104 us -> 102 us (0.981)
  Pallas kernels: 103 us -> 101 us
    pallas_call x2, Pallas kernels: 103 us -> 101 us  [the longest x1 97.9 us: local_step(): pl.pallas_call(functools.partial(kernel, chips), out_shape=out, in_specs=...]
where the time goes in v4:
time: 102 us
  Pallas kernels  101 us (99%)
    pallas_call x1, Pallas kernels, local_step(): pl.pallas_call(functools.partial(kernel, chips), out_shape=out, in_specs=...  97.9 us
    pallas_call x1, Pallas kernels, local_step(): pl.pallas_call(functools.partial(write_out, chips), out_shape=(pltpu.HBM(...  3.32 us

profile of v4, /device:TPU:113, one launch (start us, length us, event | category | flops | bytes accessed | tf_op | source)
XLA Modules:
  0.0 101.9 jit_solution(3954048978814518406)
XLA Ops:
  0.6 97.9 %shard_map.59 = (f32[64,32768]{1,0:T(8,128)S(1)}, f32[1,512]{1,0:T(1,128)S(1)}, f32[6,64,256]{2,1,0:T(8,128)S(1)}, f32[64,256]{1,0:T(8,128)S(1)}, f32[64,256]{1,0:T(8,128)S(1)}, /*index=5*/f32[8,64,256]{2,1,0:T(8,128)S(1)}) custom-call(bf16[512,6144]{1,0:T(8,128)(2,1)} %h_hbm.1, bf16[6144,4096]{1,0:T(8,128)(2,1)} %w_hbm.1, f32[1,512]{1,0:T(1,128)} %bitcast.3, ...), custom_call_target="tpu_custom_call" | custom-call | tf_op jit(solution)/shard_map/pallas_call | solution.py:362
  98.6 3.3 %shard_map.60 = (f32[64,32768]{1,0:T(8,128)}, f32[1,512]{1,0:T(1,128)}) custom-call(f32[64,32768]{1,0:T(8,128)S(1)} %get-tuple-element.10.table, f32[1,512]{1,0:T(1,128)S(1)} %get-tuple-element.11.picked, f32[6,64,256]{2,1,0:T(8,128)S(1)} %get-tuple-element.12.last, f32[64,256]{1,0:T(8,128)S(1)} %get-tuple-element.13.top, ...), custom_call_target="tpu_custom_call" | custom-call | tf_op jit(solution)/shard_map/pallas_call | solution.py:388

commit v5 on v4

--- a/solution.py
+++ b/solution.py
@@ -87,7 +87,11 @@
         return pltpu.make_async_copy(w_hbm.at[:, pl.ds(col, TILE)], w.at[slot], w_sem.at[slot])
 
     first_w = pltpu.make_async_copy(w_hbm.at[:, :LANES], w.at[0, :, :LANES], w_sem.at[1])
-    first_h = h_copy(0)
+    def far_copy(core):
+        r = pl.multiple_of((lax.rem(x + 2, chips) * 2 + core) * own, own)
+        sem = h_sem.at[chips] if core else h_sem.at[0]
+        return pltpu.make_async_copy(h_hbm.at[pl.ds(r, own), :], h.at[core * own:(core + 1) * own, :], sem)
+
     second_w = pltpu.make_async_copy(w_hbm.at[:, LANES:TILE], w.at[0, :, LANES:], w_sem.at[0])
 
     def remote(src, dst, send, recv, to):
@@ -113,10 +117,6 @@
         for i in range(remote_peers):
             send(i, t).start()
 
-    def send_half(i, half):
-        ls = slice(half * LANES, (half + 1) * LANES)
-        return remote(z.at[0, peer_rows(i), ls], land.at[i, 0, :, ls], send_sem, arrival(i, 0), peer(i))
-
     def send_stat(i):
         at = stat_out.at[CHIP_ORDER.index(PEERS[i][0])]
         return remote(at, stats.at[me], stat_send, stat_recv, peer(i))
@@ -131,7 +131,8 @@
     temp_copy = pltpu.make_async_copy(temp_hbm, temp_row, row_sem.at[0])
     ids_copy = pltpu.make_async_copy(ids_hbm, ids_row, row_sem.at[1])
     first_w.start()
-    first_h.start()
+    for core in range(2):
+        far_copy(core).start()
     temp_copy.start()
     barrier = pltpu.get_barrier_semaphore()
     for i in range(n - 1):
@@ -143,22 +144,32 @@
     temp[...] = turned(temp_row)
 
     first_w.wait()
-    first_h.wait()
-    acc = jnp.dot(h[:pair, :], w[0, :, :LANES], preferred_element_type=F32) * temp[:pair, :]
-    z[0, :pair, :LANES] = acc
-    peak[:pair, :] = acc
+    far_copy(0).wait()
+    def far_part(core, half):
+        rs, ls = slice(core * own, (core + 1) * own), slice(half * LANES, (half + 1) * LANES)
+        acc = jnp.dot(h[rs, :], w[0, :, ls], preferred_element_type=F32) * temp[rs, :]
+        z[0, rs, ls] = acc
+        peak[rs, :] = jnp.maximum(peak[rs, :], acc) if half else acc
+
+    def far_send(core, half):
+        ls = slice(half * LANES, (half + 1) * LANES)
+        slot = lax.rem(core + c, 2)
+        remote(z.at[0, core * own:(core + 1) * own, ls], land.at[slot, 0, :, ls], send_sem, recv_sem.at[slot, 0],
+               lax.rem(x + 2, chips) * 2 + core).start()
+
+    far_part(0, 0)
     pl.semaphore_wait(barrier, n - 1)
-    for i in range(2):
-        send_half(i, 0).start()
+    far_send(0, 0)
+    far_copy(1).wait()
+    far_part(1, 0)
+    far_send(1, 0)
     w_copy(1).start()
     h_copy(3).start()
     ids_copy.start()
     second_w.wait()
-    acc = jnp.dot(h[:pair, :], w[0, :, LANES:], preferred_element_type=F32) * temp[:pair, :]
-    z[0, :pair, LANES:] = acc
-    peak[:pair, :] = jnp.maximum(peak[:pair, :], acc)
-    for i in range(2):
-        send_half(i, 1).start()
+    for core in range(2):
+        far_part(core, 1)
+        far_send(core, 1)
 
     def tile_rows(t, slot, rs):
         acc = jnp.dot(h[rs, :], w[slot], preferred_element_type=F32)
@@ -379,7 +390,7 @@
                 pltpu.VMEM((chips, 1, 2 * own), F32),
                 pltpu.VMEM((2 * own, LANES), F32),
                 pltpu.VMEM((TILE, TILE), BF16),
-                dma((chips,)), dma((2,)), dma((2,)), dma, dma((n - 2, len(WAITS))), dma,
+                dma((chips + 1,)), dma((2,)), dma((2,)), dma, dma((n - 2, len(WAITS))), dma,
                 dma, dma, dma, dma,
             ],
             compiler_params=pltpu.CompilerParams(

time: 102 us -> 102 us (level)
  no operation moved by 1% of the time
where the time goes in v5:
time: 102 us; the launch traced here: 101 us
  Pallas kernels  101 us (99%)
    pallas_call x1, Pallas kernels, local_step(): pl.pallas_call(functools.partial(kernel, chips), out_shape=out, in_specs=...  97.5 us
    pallas_call x1, Pallas kernels, local_step(): pl.pallas_call(functools.partial(write_out, chips), out_shape=(pltpu.HBM(...  3.32 us

profile of v5, /device:TPU:113, one launch (start us, length us, event | category | flops | bytes accessed | tf_op | source)
XLA Modules:
  0.0 101.4 jit_solution(4169349230515702985)
XLA Ops:
  0.6 97.5 %shard_map.59 = (f32[64,32768]{1,0:T(8,128)S(1)}, f32[1,512]{1,0:T(1,128)S(1)}, f32[6,64,256]{2,1,0:T(8,128)S(1)}, f32[64,256]{1,0:T(8,128)S(1)}, f32[64,256]{1,0:T(8,128)S(1)}, /*index=5*/f32[8,64,256]{2,1,0:T(8,128)S(1)}) custom-call(bf16[512,6144]{1,0:T(8,128)(2,1)} %h_hbm.1, bf16[6144,4096]{1,0:T(8,128)(2,1)} %w_hbm.1, f32[1,512]{1,0:T(1,128)} %bitcast.3, ...), custom_call_target="tpu_custom_call" | custom-call | tf_op jit(solution)/shard_map/pallas_call | solution.py:373
  98.1 3.3 %shard_map.60 = (f32[64,32768]{1,0:T(8,128)}, f32[1,512]{1,0:T(1,128)}) custom-call(f32[64,32768]{1,0:T(8,128)S(1)} %get-tuple-element.10.table, f32[1,512]{1,0:T(1,128)S(1)} %get-tuple-element.11.picked, f32[6,64,256]{2,1,0:T(8,128)S(1)} %get-tuple-element.12.last, f32[64,256]{1,0:T(8,128)S(1)} %get-tuple-element.13.top, ...), custom_call_target="tpu_custom_call" | custom-call | tf_op jit(solution)/shard_map/pallas_call | solution.py:399

commit v6 on v5

--- a/solution.py
+++ b/solution.py
@@ -13,7 +13,7 @@
 TILE = 256
 LANES = 128
 GROUP = 4
-WAITS = (8, 7, 1)
+WAITS = (8, 4, 3, 1)
 PEERS = ((2, 0), (2, 1), (1, 0), (3, 0), (1, 1), (3, 1), (0, 1))
 CHIP_ORDER = (2, 1, 3, 0)
 
@@ -105,7 +105,7 @@
         return k
 
     def arrival(i, t):
-        return near_sem if i == remote_peers else recv_sem.at[i, counter(t)]
+        return near_sem if i == remote_peers else recv_sem.at[counter(t)]
 
     def send(i, t):
         return remote(z.at[t, peer_rows(i), :], land.at[i, t], send_sem, arrival(i, t), peer(i))
@@ -154,7 +154,7 @@
     def far_send(core, half):
         ls = slice(half * LANES, (half + 1) * LANES)
         slot = lax.rem(core + c, 2)
-        remote(z.at[0, core * own:(core + 1) * own, ls], land.at[slot, 0, :, ls], send_sem, recv_sem.at[slot, 0],
+        remote(z.at[0, core * own:(core + 1) * own, ls], land.at[slot, 0, :, ls], send_sem, recv_sem.at[0],
                lax.rem(x + 2, chips) * 2 + core).start()
 
     far_part(0, 0)
@@ -304,24 +304,17 @@
 
     for k in range(len(WAITS) - 1):
         first, size = firsts[k], WAITS[k]
-        count = min(size, 2 * GROUP - 1) if size % GROUP else GROUP
-        parts = size // count
-
-        @pl.loop(0, remote_peers * parts)
+        count = min(size, GROUP)
+        counted(land.at[pl.ds(0, remote_peers), pl.ds(first, size)], recv_sem.at[k])
+
+        @pl.loop(0, remote_peers * (size // count))
         def _(u):
-            i = lax.rem(u, remote_peers)
-            part = u // remote_peers
-
-            @pl.when(part == 0)
-            def _():
-                counted(land.at[i, pl.ds(first, size)], recv_sem.at[i, k])
-            step(i, first + part * count, count)
+            step(lax.rem(u, remote_peers), first + (u // remote_peers) * count, count)
 
     counted(pick.at[pl.ds(0, chips - 1)], pick_recv)
     for j in range(chips):
         picked[:, j * pair:(j + 1) * pair] = pick[j]
-    for i in range(remote_peers):
-        counted(last.at[i], recv_sem.at[i, len(WAITS) - 1])
+    counted(last, recv_sem.at[len(WAITS) - 1])
     counted(land, send_sem)
     counted(stats.at[pl.ds(0, n - 1)], stat_send)
     counted(pick.at[pl.ds(0, chips - 1)], pick_send)
@@ -339,8 +332,10 @@
         cs = pl.ds(pl.multiple_of(d * vocab + first, TILE), size)
         return pltpu.make_async_copy(table.at[:, cs] if source is None else source, table_hbm.at[:, cs], sem)
 
+    step = bulk // 3
     for d in range(n):
-        put(d, 0, bulk, sem.at[0]).start()
+        for k in range(3):
+            put(d, k * step, step, sem.at[0]).start()
     for d in (me, source_of(chips, x, c, n - 2)):
         put(d, bulk, TILE, sem.at[1]).start()
     picked_copy = pltpu.make_async_copy(picked, picked_hbm, sem.at[2])
@@ -390,7 +385,7 @@
                 pltpu.VMEM((chips, 1, 2 * own), F32),
                 pltpu.VMEM((2 * own, LANES), F32),
                 pltpu.VMEM((TILE, TILE), BF16),
-                dma((chips + 1,)), dma((2,)), dma((2,)), dma, dma((n - 2, len(WAITS))), dma,
+                dma((chips + 1,)), dma((2,)), dma((2,)), dma, dma((len(WAITS),)), dma,
                 dma, dma, dma, dma,
             ],
             compiler_params=pltpu.CompilerParams(

time: 102 us -> 102 us (level)
  no operation moved by 1% of the time
where the time goes in v6:
time: 102 us; the launch traced here: 101 us
  Pallas kernels  101 us (99%)
    pallas_call x1, Pallas kernels, local_step(): pl.pallas_call(functools.partial(kernel, chips), out_shape=out, in_specs=...  97.4 us
    pallas_call x1, Pallas kernels, local_step(): pl.pallas_call(functools.partial(write_out, chips), out_shape=(pltpu.HBM(...  3.29 us

profile of v6, /device:TPU:113, one launch (start us, length us, event | category | flops | bytes accessed | tf_op | source)
XLA Modules:
  0.0 101.3 jit_solution(372643212884972009)
XLA Ops:
  0.6 97.4 %shard_map.59 = (f32[64,32768]{1,0:T(8,128)S(1)}, f32[1,512]{1,0:T(1,128)S(1)}, f32[6,64,256]{2,1,0:T(8,128)S(1)}, f32[64,256]{1,0:T(8,128)S(1)}, f32[64,256]{1,0:T(8,128)S(1)}, /*index=5*/f32[8,64,256]{2,1,0:T(8,128)S(1)}) custom-call(bf16[512,6144]{1,0:T(8,128)(2,1)} %h_hbm.1, bf16[6144,4096]{1,0:T(8,128)(2,1)} %w_hbm.1, f32[1,512]{1,0:T(1,128)} %bitcast.3, ...), custom_call_target="tpu_custom_call" | custom-call | tf_op jit(solution)/shard_map/pallas_call | solution.py:368
  98.0 3.3 %shard_map.60 = (f32[64,32768]{1,0:T(8,128)}, f32[1,512]{1,0:T(1,128)}) custom-call(f32[64,32768]{1,0:T(8,128)S(1)} %get-tuple-element.10.table, f32[1,512]{1,0:T(1,128)S(1)} %get-tuple-element.11.picked, f32[6,64,256]{2,1,0:T(8,128)S(1)} %get-tuple-element.12.last, f32[64,256]{1,0:T(8,128)S(1)} %get-tuple-element.13.top, ...), custom_call_target="tpu_custom_call" | custom-call | tf_op jit(solution)/shard_map/pallas_call | solution.py:394
